TPU v7x, 32 devices: a whole 2x2x4 slice. The times are simulated.
32 devices in a mesh: band: 4 (over y, x), grid: 8 (over z, core).
Axes of the slice: x: 2, y: 2, z: 4, core: 2. Of those that a mesh axis runs over, the one named last changes fastest.
Arguments:
- wavefunctions: bfloat16 [1024, 131072], P('band', 'grid'), may hold values from -6 to 6
- projectors: bfloat16 [512, 8, 13, 256], P('grid'), may hold values from -0.0068359375 to 0.0068359375
- slot_atom: int32 [512, 8], P('grid'), may hold values from -1 to 255, as said below
- occupations: float32 [1024], P('band'), may hold values from 0.02 to 2
Outputs:
- density: float32 [256, 13, 13], P('grid')
Inputs may be any that keep to these rules, and one draw needn't show every extreme that they name: `slot_atom`: -1 marks an empty slot. Any other entry is an atom a whose owning domain a // 32 lies within 3 domains, counted around the closed cycle of 8 domains, of the domain of the block, block index // 64. In every domain some block has all 8 slots filled.
All inputs are finite; a program needn't handle non-finite values.
Results may differ from a plain program's by a relative error of at most 0.0003.
Values sent between devices are 32-bit elements; how exact they have to be, the bound alone decides.
A program may use at most 64 MiB of HBM per device.

v0:
```python
import jax
import jax.numpy as jnp
from jax import lax
from jax.sharding import PartitionSpec as P

REACH = 3
ATOMS_DEV = 32


def shifted(block, axis, distance):
    devices = range(lax.axis_size(axis))
    route = [((i - distance) % len(devices), i) for i in devices]
    return lax.ppermute(block, axis, route)


def body(wavefunctions, projectors, slot_atom, occupations):
    band_count = wavefunctions.shape[0]
    block_count, capacity, proj_count, block_len = projectors.shape
    domains = lax.axis_size("grid")
    domain = lax.axis_index("grid")
    window_len = 2 * REACH + 1
    row_len = proj_count * band_count
    grid_blocks = wavefunctions.reshape(band_count, block_count, block_len)
    stacked = projectors.reshape(block_count, capacity * proj_count, block_len)
    slot_terms = jnp.einsum(
        "ngb,gcb->gcn", grid_blocks, stacked, preferred_element_type=jnp.float32
    )
    slot_terms = slot_terms.reshape(block_count * capacity, row_len)
    slot_ids = slot_atom.reshape(-1)
    owner = jnp.floor_divide(slot_ids, ATOMS_DEV)
    offset = jnp.mod(owner - domain + REACH, domains)
    target = jnp.where(
        slot_ids >= 0, offset * ATOMS_DEV + jnp.mod(slot_ids, ATOMS_DEV), window_len * ATOMS_DEV
    )
    selector = (
        jnp.arange(window_len * ATOMS_DEV, dtype=jnp.int32)[:, None] == target[None, :]
    ).astype(jnp.float32)
    window = jnp.dot(
        selector, slot_terms, precision=lax.Precision.HIGHEST, preferred_element_type=jnp.float32
    )
    window = window.reshape(window_len, ATOMS_DEV, row_len)
    forward = window[2 * REACH]
    for hop in range(REACH, 0, -1):
        forward = shifted(forward, "grid", 1) + window[REACH + hop - 1]
    backward = window[0]
    for hop in range(REACH, 0, -1):
        addend = window[REACH - hop + 1] if hop > 1 else jnp.zeros_like(backward)
        backward = shifted(backward, "grid", -1) + addend
    owned = forward + backward
    owned = owned.reshape(ATOMS_DEV, proj_count, band_count)
    weighted = owned * occupations.reshape(1, 1, band_count)
    partial_sum = jnp.einsum("ain,ajn->aij", weighted, owned, precision=lax.Precision.HIGHEST)
    density = lax.psum(partial_sum, "band")
    return density


def solution(mesh):
    in_specs = (P("band", "grid"), P("grid", None, None, None), P("grid", None), P("band"))
    out_specs = P("grid", None, None)
    return jax.shard_map(body, mesh=mesh, in_specs=in_specs, out_specs=out_specs, check_vma=False)
```

profile of v0, /device:TPU:0, one launch (start us, length us, event | category | flops | bytes accessed | tf_op | source)
XLA Modules:
  0.0 87.4 jit_solution(6354588679132287062)
XLA Ops:
  0.0 2.8 %copy.8 = bf16[64,8,13,256]{3,0,2,1:T(8,128)(2,1)S(1)} copy(bf16[64,8,13,256]{3,1,2,0:T(8,128)(2,1)} %param.5) | data formatting | bytes 6815744 | tf_op args[1]
  2.8 9.4 %fusion = f32[64,104,256]{2,1,0:T(8,128)} fusion(bf16[32,64,8,256]{3,2,1,0:T(8,128)(2,1)} %bitcast.8, bf16[64,104,256]{2,0,1:T(8,128)(2,1)S(1)} %bitcast.7), kind=kOutput, calls=%fused_computation | convolution fusion | flops 872415232 | bytes 18612224 | tf_op jit(solution)/shard_map/ngb,gcb->gcn/dot_general | solution.py:25
  12.2 0.0 copy-start
  12.2 8.5 %reshape.103 = f32[512,3328]{1,0:T(8,128)} reshape(f32[64,104,256]{2,1,0:T(8,128)} %fusion) | data formatting | bytes 13631488 | tf_op jit(solution)/shard_map/reshape | solution.py:28
  20.7 0.0 copy-done
  20.7 0.1 copy.7
  20.7 0.1 reshape.100
  20.9 6.3 %fusion.6 = f32[224,3328]{1,0:T(8,128)S(1)} fusion(f32[512,3328]{1,0:T(8,128)} %reshape.103, s32[512]{0:T(512)S(1)} %fusion.15), kind=kOutput, calls=%fused_computation.7 | convolution fusion | flops 4580294656 | bytes 9799680 | tf_op jit(solution)/shard_map/dot_general | solution.py:38
  27.1 0.1 fusion.17
  27.2 0.5 collective-permute-start
  27.8 0.0 copy-start.1
  27.8 4.1 %collective-permute-start.3 = (f32[32,3328]{1,0:T(8,128)S(1)}, f32[32,3328]{1,0:T(8,128)S(1)}, u32[]{:S(2)}, u32[]{:S(2)}) collective-permute-start(f32[32,3328]{1,0:T(8,128)S(1)} %get-tuple-element.10), channel_id=1, source_target_pairs={{1,0},{2,1},{3,2},{4,3},{5,4},{6,5},{7,6},{0,7},{9,8},{10,9},{11,1... | collective-permute-start | bytes 1277960 | tf_op jit(solution)/shard_map/ppermute | solution.py:13
  31.9 7.7 %collective-permute-done = f32[32,3328]{1,0:T(8,128)S(1)} collective-permute-done((f32[32,3328]{1,0:T(8,128)S(1)}, f32[32,3328]{1,0:T(8,128)S(1)}, u32[]{:S(2)}, u32[]{:S(2)}) %collective-permute-start) | collective-permute-done | bytes 426016 | tf_op jit(solution)/shard_map/ppermute | solution.py:13
  39.6 0.4 collective-permute-done.3
  40.0 0.1 slice_add_fusion.4
  40.1 2.0 %collective-permute-start.1 = (f32[32,3328]{1,0:T(8,128)S(1)}, f32[32,3328]{1,0:T(8,128)S(1)}, u32[]{:S(2)}, u32[]{:S(2)}) collective-permute-start(f32[32,3328]{1,0:T(8,128)S(1)} %get-tuple-element.7), channel_id=1, source_target_pairs={{7,0},{0,1},{1,2},{2,3},{3,4},{4,5},{5,6},{6,7},{15,8},{8,9},{9,10... | collective-permute-start | bytes 1277960 | tf_op jit(solution)/shard_map/ppermute | solution.py:13
  42.1 1.8 %collective-permute-start.4 = (f32[32,3328]{1,0:T(8,128)S(1)}, f32[32,3328]{1,0:T(8,128)S(1)}, u32[]{:S(2)}, u32[]{:S(2)}) collective-permute-start(f32[32,3328]{1,0:T(8,128)S(1)} %get-tuple-element.8), channel_id=1, source_target_pairs={{1,0},{2,1},{3,2},{4,3},{5,4},{6,5},{7,6},{0,7},{9,8},{10,9},{11,1... | collective-permute-start | bytes 1277960 | tf_op jit(solution)/shard_map/ppermute | solution.py:13
  44.0 7.6 %collective-permute-done.1 = f32[32,3328]{1,0:T(8,128)S(1)} collective-permute-done((f32[32,3328]{1,0:T(8,128)S(1)}, f32[32,3328]{1,0:T(8,128)S(1)}, u32[]{:S(2)}, u32[]{:S(2)}) %collective-permute-start.1) | collective-permute-done | bytes 426016 | tf_op jit(solution)/shard_map/ppermute | solution.py:13
  51.5 0.2 collective-permute-done.4
  51.7 0.1 slice_add_fusion.3
  51.8 2.5 %collective-permute-start.2 = (f32[32,3328]{1,0:T(8,128)S(1)}, f32[32,3328]{1,0:T(8,128)S(1)}, u32[]{:S(2)}, u32[]{:S(2)}) collective-permute-start(f32[32,3328]{1,0:T(8,128)S(1)} %get-tuple-element.5), channel_id=1, source_target_pairs={{7,0},{0,1},{1,2},{2,3},{3,4},{4,5},{5,6},{6,7},{15,8},{8,9},{9,10... | collective-permute-start | bytes 1277960 | tf_op jit(solution)/shard_map/ppermute | solution.py:13
  54.2 1.4 %collective-permute-start.5 = (f32[32,3328]{1,0:T(8,128)S(1)}, f32[32,3328]{1,0:T(8,128)S(1)}, u32[]{:S(2)}, u32[]{:S(2)}) collective-permute-start(f32[32,3328]{1,0:T(8,128)S(1)} %get-tuple-element.6), channel_id=1, source_target_pairs={{1,0},{2,1},{3,2},{4,3},{5,4},{6,5},{7,6},{0,7},{9,8},{10,9},{11,1... | collective-permute-start | bytes 1277960 | tf_op jit(solution)/shard_map/ppermute | solution.py:13
  55.7 7.1 %collective-permute-done.2 = f32[32,3328]{1,0:T(8,128)S(1)} collective-permute-done((f32[32,3328]{1,0:T(8,128)S(1)}, f32[32,3328]{1,0:T(8,128)S(1)}, u32[]{:S(2)}, u32[]{:S(2)}) %collective-permute-start.2) | collective-permute-done | bytes 426016 | tf_op jit(solution)/shard_map/ppermute | solution.py:13
  62.8 1.0 %collective-permute-done.5 = f32[32,3328]{1,0:T(8,128)S(1)} collective-permute-done((f32[32,3328]{1,0:T(8,128)S(1)}, f32[32,3328]{1,0:T(8,128)S(1)}, u32[]{:S(2)}, u32[]{:S(2)}) %collective-permute-start.5) | collective-permute-done | bytes 426016 | tf_op jit(solution)/shard_map/ppermute | solution.py:13
  63.8 0.1 fusion.7
  63.9 0.1 reshape.104
  64.0 0.0 copy-done.1
  64.0 0.6 fusion.4
  64.7 21.9 %psum.7 = f32[32,13,13]{2,1,0:T(8,128)S(1)} all-reduce(f32[32,13,13]{2,1,0:T(8,128)S(1)} %fusion.4), channel_id=1, replica_groups=mesh['band'=4,'grid'=8] {'band'}, use_global_device_ids=true, to_apply=%region_0.1 | all-reduce | flops 5408 | bytes 43264 | tf_op jit(solution)/shard_map/psum | solution.py:53
  86.6 0.8 copy.11
  (1 shorter events, 0.0 us)
Async XLA Ops:
  12.2 8.5 %copy-start = (s32[64,8]{0,1:T(8,128)S(1)}, s32[64,8]{0,1:T(8,128)}, u32[]{:S(2)}) copy-start(s32[64,8]{0,1:T(8,128)} %param.6) | copy-start | bytes 6148
  27.2 12.3 %collective-permute-start = (f32[32,3328]{1,0:T(8,128)S(1)}, f32[32,3328]{1,0:T(8,128)S(1)}, u32[]{:S(2)}, u32[]{:S(2)}) collective-permute-start(f32[32,3328]{1,0:T(8,128)S(1)} %get-tuple-element.9), channel_id=1, source_target_pairs={{7,0},{0,1},{1,2},{2,3},{3,4},{4,5},{5,6},{6,7},{15,8},{8,9},{9,10... | collective-permute-start | bytes 1277960 | tf_op jit(solution)/shard_map/ppermute | solution.py:13
  27.8 36.3 %copy-start.1 = (f32[256]{0:T(256)S(1)}, f32[256]{0:T(256)}, u32[]{:S(2)}) copy-start(f32[256]{0:T(256)} %param.7) | copy-start | bytes 3076
  27.8 12.2 %collective-permute-start.3 = (f32[32,3328]{1,0:T(8,128)S(1)}, f32[32,3328]{1,0:T(8,128)S(1)}, u32[]{:S(2)}, u32[]{:S(2)}) collective-permute-start(f32[32,3328]{1,0:T(8,128)S(1)} %get-tuple-element.10), channel_id=1, source_target_pairs={{1,0},{2,1},{3,2},{4,3},{5,4},{6,5},{7,6},{0,7},{9,8},{10,9},{11,1... | collective-permute-start | bytes 1277960 | tf_op jit(solution)/shard_map/ppermute | solution.py:13
  40.1 11.5 %collective-permute-start.1 = (f32[32,3328]{1,0:T(8,128)S(1)}, f32[32,3328]{1,0:T(8,128)S(1)}, u32[]{:S(2)}, u32[]{:S(2)}) collective-permute-start(f32[32,3328]{1,0:T(8,128)S(1)} %get-tuple-element.7), channel_id=1, source_target_pairs={{7,0},{0,1},{1,2},{2,3},{3,4},{4,5},{5,6},{6,7},{15,8},{8,9},{9,10... | collective-permute-start | bytes 1277960 | tf_op jit(solution)/shard_map/ppermute | solution.py:13
  42.1 9.6 %collective-permute-start.4 = (f32[32,3328]{1,0:T(8,128)S(1)}, f32[32,3328]{1,0:T(8,128)S(1)}, u32[]{:S(2)}, u32[]{:S(2)}) collective-permute-start(f32[32,3328]{1,0:T(8,128)S(1)} %get-tuple-element.8), channel_id=1, source_target_pairs={{1,0},{2,1},{3,2},{4,3},{5,4},{6,5},{7,6},{0,7},{9,8},{10,9},{11,1... | collective-permute-start | bytes 1277960 | tf_op jit(solution)/shard_map/ppermute | solution.py:13
  51.8 11.0 %collective-permute-start.2 = (f32[32,3328]{1,0:T(8,128)S(1)}, f32[32,3328]{1,0:T(8,128)S(1)}, u32[]{:S(2)}, u32[]{:S(2)}) collective-permute-start(f32[32,3328]{1,0:T(8,128)S(1)} %get-tuple-element.5), channel_id=1, source_target_pairs={{7,0},{0,1},{1,2},{2,3},{3,4},{4,5},{5,6},{6,7},{15,8},{8,9},{9,10... | collective-permute-start | bytes 1277960 | tf_op jit(solution)/shard_map/ppermute | solution.py:13
  54.2 9.6 %collective-permute-start.5 = (f32[32,3328]{1,0:T(8,128)S(1)}, f32[32,3328]{1,0:T(8,128)S(1)}, u32[]{:S(2)}, u32[]{:S(2)}) collective-permute-start(f32[32,3328]{1,0:T(8,128)S(1)} %get-tuple-element.6), channel_id=1, source_target_pairs={{1,0},{2,1},{3,2},{4,3},{5,4},{6,5},{7,6},{0,7},{9,8},{10,9},{11,1... | collective-permute-start | bytes 1277960 | tf_op jit(solution)/shard_map/ppermute | solution.py:13
where the time goes:
time: 87.8 us; the launch traced here: 87.4 us
  waiting for transfers between devices  24 us (27%)
  blocking collectives  21.9 us (25%)
  matrix products  16.3 us (19%)
  local copies, waits for them, and re-layouts  12.4 us (14%)
  starting transfers between devices  12.4 us (14%)
    ppermute x6, waiting for transfers between devices, shifted(): return lax.ppermute(block, axis, route)  24 us
    psum x1, blocking collectives, body(): density = lax.psum(partial_sum, 'band')  21.9 us
    ppermute x6, starting transfers between devices, shifted(): return lax.ppermute(block, axis, route)  12.4 us
    dot_general x1, matrix products, body(): jnp.einsum('ngb,gcb->gcn', grid_blocks, stacked, preferred_element_type=j...  9.38 us
    reshape x1, local copies, waits for them, and re-layouts, body(): slot_terms = slot_terms.reshape(block_count * capacity, row_len)  8.49 us
    dot_general x1, matrix products, body(): jnp.dot(selector, slot_terms, precision=lax.Precision.HIGHEST, preferred_...  6.29 us
    unnamed x6, local copies, waits for them, and re-layouts  2.86 us
  transfers between devices with their start and end apart: 6, of which 6 were waited for; matrix products, arithmetic and copies ran while one was open for 0% of the time, Pallas kernels for 0%

commit v1 on v0

--- a/solution.py
+++ b/solution.py
@@ -50,7 +50,7 @@
     owned = owned.reshape(ATOMS_DEV, proj_count, band_count)
     weighted = owned * occupations.reshape(1, 1, band_count)
     partial_sum = jnp.einsum("ain,ajn->aij", weighted, owned, precision=lax.Precision.HIGHEST)
-    density = lax.psum(partial_sum, "band")
+    density = jnp.sum(lax.all_gather(partial_sum, "band"), axis=0)
     return density
 
 

time: 87.8 us -> 81.2 us (0.925)
  blocking collectives: 21.9 us -> 15.2 us
    psum x1 -> x0, blocking collectives: 21.9 us -> none  [body(): density = lax.psum(partial_sum, 'band')]
    all_gather x0 -> x1, blocking collectives: none -> 15.2 us  [body(): density = jnp.sum(lax.all_gather(partial_sum, 'band'), axis=0)]
where the time goes in v1:
time: 81.2 us; the launch traced here: 80.8 us
  waiting for transfers between devices  24 us (30%)
  matrix products  16.3 us (20%)
  blocking collectives  15.2 us (19%)
  local copies, waits for them, and re-layouts  12.4 us (15%)
  starting transfers between devices  12.4 us (15%)
    ppermute x6, waiting for transfers between devices, shifted(): return lax.ppermute(block, axis, route)  24 us
    all_gather x1, blocking collectives, body(): density = jnp.sum(lax.all_gather(partial_sum, 'band'), axis=0)  15.2 us
    ppermute x6, starting transfers between devices, shifted(): return lax.ppermute(block, axis, route)  12.4 us
    dot_general x1, matrix products, body(): jnp.einsum('ngb,gcb->gcn', grid_blocks, stacked, preferred_element_type=j...  9.38 us
    reshape x1, local copies, waits for them, and re-layouts, body(): slot_terms = slot_terms.reshape(block_count * capacity, row_len)  8.49 us
    dot_general x1, matrix products, body(): jnp.dot(selector, slot_terms, precision=lax.Precision.HIGHEST, preferred_...  6.29 us
    unnamed x6, local copies, waits for them, and re-layouts  2.86 us
  transfers between devices with their start and end apart: 6, of which 6 were waited for; matrix products, arithmetic and copies ran while one was open for 0% of the time, Pallas kernels for 0%

profile of v1, /device:TPU:0, one launch (start us, length us, event | category | flops | bytes accessed | tf_op | source)
XLA Modules:
  0.0 80.8 jit_solution(10281824514119819824)
XLA Ops:
  0.0 2.8 %copy.11 = bf16[64,8,13,256]{3,0,2,1:T(8,128)(2,1)S(1)} copy(bf16[64,8,13,256]{3,1,2,0:T(8,128)(2,1)} %param.5) | data formatting | bytes 6815744 | tf_op args[1]
  2.8 9.4 %fusion = f32[64,104,256]{2,1,0:T(8,128)} fusion(bf16[32,64,8,256]{3,2,1,0:T(8,128)(2,1)} %bitcast.9, bf16[64,104,256]{2,0,1:T(8,128)(2,1)S(1)} %bitcast.8), kind=kOutput, calls=%fused_computation | convolution fusion | flops 872415232 | bytes 18612224 | tf_op jit(solution)/shard_map/ngb,gcb->gcn/dot_general | solution.py:25
  12.2 0.0 copy-start
  12.2 8.5 %reshape.103 = f32[512,3328]{1,0:T(8,128)} reshape(f32[64,104,256]{2,1,0:T(8,128)} %fusion) | data formatting | bytes 13631488 | tf_op jit(solution)/shard_map/reshape | solution.py:28
  20.7 0.0 copy-done
  20.7 0.1 copy.10
  20.7 0.1 reshape.100
  20.9 6.3 %fusion.6 = f32[224,3328]{1,0:T(8,128)S(1)} fusion(f32[512,3328]{1,0:T(8,128)} %reshape.103, s32[512]{0:T(512)S(1)} %fusion.15), kind=kOutput, calls=%fused_computation.7 | convolution fusion | flops 4580294656 | bytes 9799680 | tf_op jit(solution)/shard_map/dot_general | solution.py:38
  27.1 0.1 fusion.17
  27.2 0.5 collective-permute-start
  27.8 0.0 copy-start.1
  27.8 4.1 %collective-permute-start.3 = (f32[32,3328]{1,0:T(8,128)S(1)}, f32[32,3328]{1,0:T(8,128)S(1)}, u32[]{:S(2)}, u32[]{:S(2)}) collective-permute-start(f32[32,3328]{1,0:T(8,128)S(1)} %get-tuple-element.10), channel_id=1, source_target_pairs={{1,0},{2,1},{3,2},{4,3},{5,4},{6,5},{7,6},{0,7},{9,8},{10,9},{11,1... | collective-permute-start | bytes 1277960 | tf_op jit(solution)/shard_map/ppermute | solution.py:13
  31.9 7.7 %collective-permute-done = f32[32,3328]{1,0:T(8,128)S(1)} collective-permute-done((f32[32,3328]{1,0:T(8,128)S(1)}, f32[32,3328]{1,0:T(8,128)S(1)}, u32[]{:S(2)}, u32[]{:S(2)}) %collective-permute-start) | collective-permute-done | bytes 426016 | tf_op jit(solution)/shard_map/ppermute | solution.py:13
  39.6 0.4 collective-permute-done.3
  40.0 0.1 slice_add_fusion.4
  40.1 2.0 %collective-permute-start.1 = (f32[32,3328]{1,0:T(8,128)S(1)}, f32[32,3328]{1,0:T(8,128)S(1)}, u32[]{:S(2)}, u32[]{:S(2)}) collective-permute-start(f32[32,3328]{1,0:T(8,128)S(1)} %get-tuple-element.7), channel_id=1, source_target_pairs={{7,0},{0,1},{1,2},{2,3},{3,4},{4,5},{5,6},{6,7},{15,8},{8,9},{9,10... | collective-permute-start | bytes 1277960 | tf_op jit(solution)/shard_map/ppermute | solution.py:13
  42.1 1.8 %collective-permute-start.4 = (f32[32,3328]{1,0:T(8,128)S(1)}, f32[32,3328]{1,0:T(8,128)S(1)}, u32[]{:S(2)}, u32[]{:S(2)}) collective-permute-start(f32[32,3328]{1,0:T(8,128)S(1)} %get-tuple-element.8), channel_id=1, source_target_pairs={{1,0},{2,1},{3,2},{4,3},{5,4},{6,5},{7,6},{0,7},{9,8},{10,9},{11,1... | collective-permute-start | bytes 1277960 | tf_op jit(solution)/shard_map/ppermute | solution.py:13
  44.0 7.6 %collective-permute-done.1 = f32[32,3328]{1,0:T(8,128)S(1)} collective-permute-done((f32[32,3328]{1,0:T(8,128)S(1)}, f32[32,3328]{1,0:T(8,128)S(1)}, u32[]{:S(2)}, u32[]{:S(2)}) %collective-permute-start.1) | collective-permute-done | bytes 426016 | tf_op jit(solution)/shard_map/ppermute | solution.py:13
  51.5 0.2 collective-permute-done.4
  51.7 0.1 slice_add_fusion.3
  51.8 2.5 %collective-permute-start.2 = (f32[32,3328]{1,0:T(8,128)S(1)}, f32[32,3328]{1,0:T(8,128)S(1)}, u32[]{:S(2)}, u32[]{:S(2)}) collective-permute-start(f32[32,3328]{1,0:T(8,128)S(1)} %get-tuple-element.5), channel_id=1, source_target_pairs={{7,0},{0,1},{1,2},{2,3},{3,4},{4,5},{5,6},{6,7},{15,8},{8,9},{9,10... | collective-permute-start | bytes 1277960 | tf_op jit(solution)/shard_map/ppermute | solution.py:13
  54.2 1.4 %collective-permute-start.5 = (f32[32,3328]{1,0:T(8,128)S(1)}, f32[32,3328]{1,0:T(8,128)S(1)}, u32[]{:S(2)}, u32[]{:S(2)}) collective-permute-start(f32[32,3328]{1,0:T(8,128)S(1)} %get-tuple-element.6), channel_id=1, source_target_pairs={{1,0},{2,1},{3,2},{4,3},{5,4},{6,5},{7,6},{0,7},{9,8},{10,9},{11,1... | collective-permute-start | bytes 1277960 | tf_op jit(solution)/shard_map/ppermute | solution.py:13
  55.7 7.1 %collective-permute-done.2 = f32[32,3328]{1,0:T(8,128)S(1)} collective-permute-done((f32[32,3328]{1,0:T(8,128)S(1)}, f32[32,3328]{1,0:T(8,128)S(1)}, u32[]{:S(2)}, u32[]{:S(2)}) %collective-permute-start.2) | collective-permute-done | bytes 426016 | tf_op jit(solution)/shard_map/ppermute | solution.py:13
  62.8 1.0 %collective-permute-done.5 = f32[32,3328]{1,0:T(8,128)S(1)} collective-permute-done((f32[32,3328]{1,0:T(8,128)S(1)}, f32[32,3328]{1,0:T(8,128)S(1)}, u32[]{:S(2)}, u32[]{:S(2)}) %collective-permute-start.5) | collective-permute-done | bytes 426016 | tf_op jit(solution)/shard_map/ppermute | solution.py:13
  63.8 0.1 fusion.7
  63.9 0.1 reshape.104
  64.0 0.0 copy-done.1
  64.0 0.6 fusion.4
  64.7 15.2 %all-gather = f32[128,13,13]{2,1,0:T(8,128)S(1)} all-gather(f32[32,13,13]{2,1,0:T(8,128)S(1)} %fusion.4), channel_id=2, replica_groups=mesh['band'=4,'grid'=8] {'band'}, dimensions={0}, use_global_device_ids=true | all-gather | bytes 108160 | tf_op jit(solution)/shard_map/all_gather | solution.py:53
  79.9 0.1 reduce_sum.9
  80.0 0.8 %copy.14 = f32[32,13,13]{0,2,1:T(8,128)} copy(f32[32,13,13]{2,1,0:T(8,128)S(1)} %reduce_sum.9) | data formatting | bytes 43264 | tf_op jit(solution)/shard_map/reduce_sum | solution.py:53
  (1 shorter events, 0.0 us)
Async XLA Ops:
  12.2 8.5 %copy-start = (s32[64,8]{0,1:T(8,128)S(1)}, s32[64,8]{0,1:T(8,128)}, u32[]{:S(2)}) copy-start(s32[64,8]{0,1:T(8,128)} %param.6) | copy-start | bytes 6148
  27.2 12.3 %collective-permute-start = (f32[32,3328]{1,0:T(8,128)S(1)}, f32[32,3328]{1,0:T(8,128)S(1)}, u32[]{:S(2)}, u32[]{:S(2)}) collective-permute-start(f32[32,3328]{1,0:T(8,128)S(1)} %get-tuple-element.9), channel_id=1, source_target_pairs={{7,0},{0,1},{1,2},{2,3},{3,4},{4,5},{5,6},{6,7},{15,8},{8,9},{9,10... | collective-permute-start | bytes 1277960 | tf_op jit(solution)/shard_map/ppermute | solution.py:13
  27.8 36.3 %copy-start.1 = (f32[256]{0:T(256)S(1)}, f32[256]{0:T(256)}, u32[]{:S(2)}) copy-start(f32[256]{0:T(256)} %param.7) | copy-start | bytes 3076
  27.8 12.2 %collective-permute-start.3 = (f32[32,3328]{1,0:T(8,128)S(1)}, f32[32,3328]{1,0:T(8,128)S(1)}, u32[]{:S(2)}, u32[]{:S(2)}) collective-permute-start(f32[32,3328]{1,0:T(8,128)S(1)} %get-tuple-element.10), channel_id=1, source_target_pairs={{1,0},{2,1},{3,2},{4,3},{5,4},{6,5},{7,6},{0,7},{9,8},{10,9},{11,1... | collective-permute-start | bytes 1277960 | tf_op jit(solution)/shard_map/ppermute | solution.py:13
  40.1 11.5 %collective-permute-start.1 = (f32[32,3328]{1,0:T(8,128)S(1)}, f32[32,3328]{1,0:T(8,128)S(1)}, u32[]{:S(2)}, u32[]{:S(2)}) collective-permute-start(f32[32,3328]{1,0:T(8,128)S(1)} %get-tuple-element.7), channel_id=1, source_target_pairs={{7,0},{0,1},{1,2},{2,3},{3,4},{4,5},{5,6},{6,7},{15,8},{8,9},{9,10... | collective-permute-start | bytes 1277960 | tf_op jit(solution)/shard_map/ppermute | solution.py:13
  42.1 9.6 %collective-permute-start.4 = (f32[32,3328]{1,0:T(8,128)S(1)}, f32[32,3328]{1,0:T(8,128)S(1)}, u32[]{:S(2)}, u32[]{:S(2)}) collective-permute-start(f32[32,3328]{1,0:T(8,128)S(1)} %get-tuple-element.8), channel_id=1, source_target_pairs={{1,0},{2,1},{3,2},{4,3},{5,4},{6,5},{7,6},{0,7},{9,8},{10,9},{11,1... | collective-permute-start | bytes 1277960 | tf_op jit(solution)/shard_map/ppermute | solution.py:13
  51.8 11.0 %collective-permute-start.2 = (f32[32,3328]{1,0:T(8,128)S(1)}, f32[32,3328]{1,0:T(8,128)S(1)}, u32[]{:S(2)}, u32[]{:S(2)}) collective-permute-start(f32[32,3328]{1,0:T(8,128)S(1)} %get-tuple-element.5), channel_id=1, source_target_pairs={{7,0},{0,1},{1,2},{2,3},{3,4},{4,5},{5,6},{6,7},{15,8},{8,9},{9,10... | collective-permute-start | bytes 1277960 | tf_op jit(solution)/shard_map/ppermute | solution.py:13
  54.2 9.6 %collective-permute-start.5 = (f32[32,3328]{1,0:T(8,128)S(1)}, f32[32,3328]{1,0:T(8,128)S(1)}, u32[]{:S(2)}, u32[]{:S(2)}) collective-permute-start(f32[32,3328]{1,0:T(8,128)S(1)} %get-tuple-element.6), channel_id=1, source_target_pairs={{1,0},{2,1},{3,2},{4,3},{5,4},{6,5},{7,6},{0,7},{9,8},{10,9},{11,1... | collective-permute-start | bytes 1277960 | tf_op jit(solution)/shard_map/ppermute | solution.py:13
